TPU v7x, 32 devices: a whole 2x2x4 slice. The times are simulated.
32 devices in a mesh: stream: 16 (over z, y, core), tm: 2 (over x).
Axes of the slice: x: 2, y: 2, z: 4, core: 2. Of those that a mesh axis runs over, the one named last changes fastest.
Arguments:
- signal: bfloat16 [32, 2, 1048576], P('stream', None, 'tm'), parts along dimension 0, may hold values from -11 to 11
- taps: float32 [16, 4096], replicated, may hold values from -1.5 to 1.5
Outputs:
- channels_out: float32 [32, 2, 4096, 256], P('stream', None, 'tm'), parts along dimension 0
There are 16 independent parts, one for each index of `stream`. A program takes and returns all parts, laid end to end along the dimension named above; an argument that names none is the same for every part. Nothing has to cross between parts.
All inputs are finite; a program needn't handle non-finite values.
Results may differ from a plain program's by a relative error of at most 0.0003.
Values may be sent and summed in bfloat16 or wider, within the bound.
A program may use at most 128 MiB of HBM per device.

v0:
```python
import functools
import math

import jax
import jax.numpy as jnp
import numpy as np
from jax import lax
from jax.experimental import pallas as pl
from jax.experimental.pallas import tpu as pltpu
from jax.sharding import PartitionSpec as P

LANES = 128
GROUP = 4
PAIR = 2 * GROUP


def angles(height, breadth, modulus):
    product = np.arange(height)[:, None] * np.arange(breadth)[None, :] % modulus
    return product * (2.0 * math.pi / modulus)


def split(table):
    high = table.astype(np.float32).astype(jnp.bfloat16)
    low = (table - high.astype(np.float64)).astype(np.float32).astype(jnp.bfloat16)
    return high, low


def first_table(rows):
    turn = angles(rows, rows, rows)
    cos, sin = np.cos(turn), np.sin(turn)
    whole = np.block([[cos, sin], [-sin, cos]])
    high, low = split(np.kron(np.eye(GROUP), whole))
    return np.concatenate([high, low, high], axis=1)


def second_table(rows, channels, parts):
    turn = angles(LANES, LANES, LANES)
    scale = 1.0 / math.isqrt(channels)
    cos, sin = np.cos(turn) * scale, np.sin(turn) * scale
    each = LANES // parts
    blocks = []
    for part in range(parts):
        pick = slice(part * each, (part + 1) * each)
        blocks.append(np.block([[cos[pick], sin[pick]], [-sin[pick], cos[pick]]]))
    high, low = split(np.concatenate(blocks, axis=0))
    return np.concatenate([high, low, high], axis=1)


def transform_kernel(parts, frames, rows, edge, x_ref, halo_ref, taps_ref, first_ref, cos_ref,
                     sin_ref, second_ref, own_ref, away_ref, wide, grid, zr, zi):
    depth = edge
    for p in range(2):
        wide[p, :edge] = halo_ref[0, p].astype(jnp.float32)

    @pl.loop(0, frames // PAIR)
    def _(step):
        base = pl.multiple_of(step * PAIR, PAIR)
        for p in range(2):
            wide[p, pl.ds(base + edge, PAIR)] = x_ref[0, p, pl.ds(base, PAIR)].astype(jnp.float32)

    @pl.loop(0, frames // PAIR)
    def _(step):
        base = pl.multiple_of(step * PAIR, PAIR)
        for p in range(2):
            for piece in range(rows // 8):
                sub = slice(piece * 8, piece * 8 + 8)
                data = [wide[p, base + 1 + i, sub, :] for i in range(PAIR + depth - 1)]
                taps = [taps_ref[k, sub, :] for k in range(depth)]
                for t in range(PAIR):
                    total = taps[0] * data[t + depth - 1]
                    for k in range(1, depth):
                        total = total + taps[k] * data[t + depth - 1 - k]
                    row = ((t % GROUP) * 2 + p) * rows + piece * 8
                    lane = (t // GROUP) * LANES
                    grid[row : row + 8, lane : lane + LANES] = total
        value = grid[...]
        high = value.astype(jnp.bfloat16)
        low = (value - high.astype(jnp.float32)).astype(jnp.bfloat16)
        out = jnp.dot(first_ref[...], jnp.concatenate([high, high, low], axis=0),
                      preferred_element_type=jnp.float32)
        cos, sin = cos_ref[...], sin_ref[...]
        for t in range(PAIR):
            row = (t % GROUP) * 2 * rows
            lane = (t // GROUP) * LANES
            real = out[row : row + rows, lane : lane + LANES]
            imag = out[row + rows : row + 2 * rows, lane : lane + LANES]
            at = pl.multiple_of((base + t) * rows, rows)
            zr[pl.ds(at, rows), :] = real * cos + imag * sin
            zi[pl.ds(at, rows), :] = imag * cos - real * sin

    each = LANES // parts

    @pl.loop(0, rows // 2)
    def _(step):
        pieces = []
        for i in range(2):
            pick = pl.ds(step * 2 + i, frames, stride=rows)
            pieces.append(jnp.concatenate([zr[pick, :], zi[pick, :]], axis=1))
        value = jnp.concatenate(pieces, axis=0)
        high = value.astype(jnp.bfloat16)
        low = (value - high.astype(jnp.float32)).astype(jnp.bfloat16)
        out = lax.dot_general(second_ref[...], jnp.concatenate([high, high, low], axis=1),
                              (((1,), (1,)), ((), ())), preferred_element_type=jnp.float32)
        for i in range(2):
            c = step * 2 + i
            lane = slice(i * frames, (i + 1) * frames)
            for p in range(2):
                own_ref[p, c] = out[p * each : (p + 1) * each, lane]
                for k in range(1, parts):
                    top = (2 * k + p) * each
                    away_ref[k - 1, p, c] = out[top : top + each, lane]


def finish_kernel(parts, frames, rows, each, *refs):
    own_ref, away_refs, out_ref, turned = refs[0], refs[1:parts], refs[-2], refs[-1]
    me = lax.axis_index("tm")

    @pl.loop(0, rows)
    def _(c):
        data = [[own_ref[p, c] for p in range(2)]]
        for ref in away_refs:
            data.append([ref[p, c] for p in range(2)])
        square = sum(d[0] * d[0] + d[1] * d[1] for d in data)
        power = jnp.sum(square, axis=1, keepdims=True)
        factor = lax.rsqrt(power * (1.0 / (frames * parts)) + 1.0)
        for k in range(parts):
            for p in range(2):
                turned[k, p, pl.ds(c, each, stride=rows), :] = data[k][p] * factor

    for k in range(parts):
        source = lax.rem(me + parts - k, parts)
        lane = pl.ds(pl.multiple_of(source * frames, frames), frames)
        for p in range(2):
            out_ref[0, p, :, lane] = turned[k, p]


def sent(block, route):
    narrow = (block * 2.0).astype(jnp.float16)
    return lax.ppermute(narrow, "tm", route).astype(jnp.float32) * 0.5


def shards(parts, signal, taps):
    streams = signal.shape[0]
    depth, channels = taps.shape
    rows = channels // LANES
    frames = signal.shape[2] // channels
    each = LANES // parts
    me = lax.axis_index("tm")
    x = signal.reshape(streams, 2, frames, rows, LANES)
    route = [(i, i + 1) for i in range(parts - 1)]
    halo = lax.ppermute(x[:, :, frames - depth :], "tm", route)
    taps = taps.reshape(depth, rows, LANES)
    twist = angles(rows, LANES, channels)
    cos, sin = jnp.asarray(np.cos(twist), jnp.float32), jnp.asarray(np.sin(twist), jnp.float32)
    first = jnp.asarray(first_table(rows))
    table = second_table(rows, channels, parts)
    second = lax.dynamic_slice(
        jnp.asarray(np.concatenate([table, table], axis=0)),
        (me * 2 * each, 0), table.shape)
    owns, aways = [], []
    whole = lambda a: pl.BlockSpec(a.shape, lambda i, nd=a.ndim: (0,) * nd)
    for s in range(streams):
        pick = lambda i, s=s: (s, 0, 0, 0, 0)
        own, away = pl.pallas_call(
            functools.partial(transform_kernel, parts, frames, rows, depth),
            grid=(1,),
            in_specs=[
                pl.BlockSpec((1, 2, frames, rows, LANES), pick),
                pl.BlockSpec((1, 2, depth, rows, LANES), pick),
                whole(taps), whole(first), whole(cos), whole(sin), whole(second),
            ],
            out_specs=[
                pl.BlockSpec((2, rows, each, frames), lambda i: (0, 0, 0, 0)),
                pl.BlockSpec((parts - 1, 2, rows, each, frames), lambda i: (0, 0, 0, 0, 0)),
            ],
            out_shape=[
                jax.ShapeDtypeStruct((2, rows, each, frames), jnp.float32),
                jax.ShapeDtypeStruct((parts - 1, 2, rows, each, frames), jnp.float32),
            ],
            scratch_shapes=[
                pltpu.VMEM((2, depth + frames, rows, LANES), jnp.float32),
                pltpu.VMEM((2 * GROUP * rows, 2 * LANES), jnp.float32),
                pltpu.VMEM((frames * rows, LANES), jnp.float32),
                pltpu.VMEM((frames * rows, LANES), jnp.float32),
            ],
            compiler_params=pltpu.CompilerParams(vmem_limit_bytes=48 << 20),
            cost_estimate=pl.CostEstimate(flops=8 * 10**9, bytes_accessed=8 << 20, transcendentals=0),
            name="transform",
        )(x, halo, taps, first, cos, sin, second)
        owns.append(own)
        aways.append([
            sent(away[k - 1], [(i, (i + k) % parts) for i in range(parts)])
            for k in range(1, parts)
        ])
    result = None
    step = 16
    shape = jax.ShapeDtypeStruct((streams, 2, channels // parts, frames * parts), jnp.float32)
    for s in range(streams):
        block = pl.BlockSpec((2, rows, step, frames), lambda i: (0, 0, i, 0))
        args = [owns[s], *aways[s]]
        specs = [block] * parts
        alias = {}
        if result is not None:
            alias = {len(args): 0}
            args.append(result)
            specs.append(pl.BlockSpec(memory_space=pl.ANY))
        result = pl.pallas_call(
            functools.partial(finish_kernel, parts, frames, rows, step),
            grid=(each // step,),
            in_specs=specs,
            out_specs=pl.BlockSpec((1, 2, rows * step, frames * parts), lambda i, s=s: (s, 0, i, 0)),
            out_shape=shape,
            input_output_aliases=alias,
            scratch_shapes=[pltpu.VMEM((parts, 2, rows * step, frames), jnp.float32)],
            compiler_params=pltpu.CompilerParams(vmem_limit_bytes=48 << 20),
            cost_estimate=pl.CostEstimate(flops=10**8, bytes_accessed=8 << 20, transcendentals=0),
            name="finish",
        )(*args)
    return result


def solution(mesh):
    in_specs = (P("stream", None, "tm"), P())
    out_specs = P("stream", None, "tm", None)
    body = functools.partial(shards, mesh.shape["tm"])
    return jax.shard_map(body, mesh=mesh, in_specs=in_specs, out_specs=out_specs, check_vma=False)
```

profile of v0, /device:TPU:0, one launch (start us, length us, event | category | flops | bytes accessed | tf_op | source)
XLA Modules:
  0.0 107.4 jit_solution(15759912410660161400)
XLA Ops:
  0.0 0.0 copy-start.4
  0.0 0.0 copy-start.3
  0.0 6.1 %reshape.12.x_ref = bf16[2,2,128,32,128]{4,3,2,1,0:T(8,128)(2,1)} reshape(bf16[2,2,524288]{2,1,0:T(2,128)(2,1)} %param.6) | data formatting | bytes 8388608 | tf_op jit(solution)/shard_map/reshape | solution.py:149
  6.1 1.1 %slice.4 = bf16[2,2,16,32,128]{4,3,2,1,0:T(8,128)(2,1)S(1)} slice(bf16[2,2,128,32,128]{4,3,2,1,0:T(8,128)(2,1)} %reshape.12.x_ref), slice={[0:2], [0:2], [112:128], [0:32], [0:128]} | slice | bytes 1048576 | tf_op jit(solution)/shard_map/slice | solution.py:151
  7.3 4.9 %collective-permute-start = (bf16[2,2,16,32,128]{4,3,2,1,0:T(8,128)(2,1)S(1)}, bf16[2,2,16,32,128]{4,3,2,1,0:T(8,128)(2,1)S(1)}, u32[]{:S(2)}, u32[]{:S(2)}) collective-permute-start(bf16[2,2,16,32,128]{4,3,2,1,0:T(8,128)(2,1)S(1)} %slice.4), channel_id=1, source_target_pairs={{0,1},{2,3},{4,5},{6,7},{8,9},{10,11},{12,13},{14,15},{16,17},{18,... | collective-permute-start | bytes 1572872 | tf_op jit(solution)/shard_map/ppermute | solution.py:151
  12.2 0.0 copy-done.3
  12.2 0.1 copy.8
  12.2 0.0 copy-done.4
  12.3 11.0 %collective-permute-done.halo_ref = bf16[2,2,16,32,128]{4,3,2,1,0:T(8,128)(2,1)S(1)} collective-permute-done((bf16[2,2,16,32,128]{4,3,2,1,0:T(8,128)(2,1)S(1)}, bf16[2,2,16,32,128]{4,3,2,1,0:T(8,128)(2,1)S(1)}, u32[]{:S(2)}, u32[]{:S(2)}) %collective-permute-start) | collective-permute-done | bytes 524320 | tf_op jit(solution)/shard_map/ppermute | solution.py:151
  23.3 0.0 copy-done
  23.3 0.0 copy-done.1
  23.3 0.0 copy-done.2
  23.3 19.0 %transform.3 = (f32[2,32,64,128]{3,2,1,0:T(8,128)S(1)}, f32[1,2,32,64,128]{4,3,2,1,0:T(8,128)S(1)}) custom-call(bf16[2,2,128,32,128]{4,3,2,1,0:T(8,128)(2,1)} %reshape.12.x_ref, bf16[2,2,16,32,128]{4,3,2,1,0:T(8,128)(2,1)S(1)} %collective-permute-done.halo_ref, f32[16,32,128]{2,1,0:T(8,128)S(1)} %bitcast.6, bf16[256,768]{1,0:T(8,128)(2,1)S(1)} %copy-done, ...), custom_call_target="tpu_custom_call" | custom-call | flops 8000000000 | bytes 8388608 | tf_op jit(solution)/shard_map/transform/pallas_call | solution.py:164
  42.3 0.3 fusion.1
  42.6 2.5 %collective-permute-start.2 = (f16[2,32,64,128]{3,2,1,0:T(8,128)(2,1)S(1)}, f16[2,32,64,128]{3,2,1,0:T(8,128)(2,1)S(1)}, u32[]{:S(2)}, u32[]{:S(2)}) collective-permute-start(f16[2,32,64,128]{3,2,1,0:T(8,128)(2,1)S(1)} %fusion.1), channel_id=1, source_target_pairs={{0,1},{1,0},{2,3},{3,2},{4,5},{5,4},{6,7},{7,6},{8,9},{9,8},{10,11... | collective-permute-start | bytes 3145736 | tf_op jit(solution)/shard_map/ppermute | solution.py:139
  45.1 19.0 %transform.2 = (f32[2,32,64,128]{3,2,1,0:T(8,128)S(1)}, f32[1,2,32,64,128]{4,3,2,1,0:T(8,128)S(1)}) custom-call(bf16[2,2,128,32,128]{4,3,2,1,0:T(8,128)(2,1)} %reshape.12.x_ref, bf16[2,2,16,32,128]{4,3,2,1,0:T(8,128)(2,1)S(1)} %collective-permute-done.halo_ref, f32[16,32,128]{2,1,0:T(8,128)S(1)} %bitcast.7, bf16[256,768]{1,0:T(8,128)(2,1)S(1)} %copy-done, ...), custom_call_target="tpu_custom_call" | custom-call | flops 8000000000 | bytes 8388608 | tf_op jit(solution)/shard_map/transform/pallas_call | solution.py:164
  64.1 0.3 fusion
  64.4 0.1 collective-permute-start.1
  64.5 4.5 %collective-permute-done.2 = f16[2,32,64,128]{3,2,1,0:T(8,128)(2,1)S(1)} collective-permute-done((f16[2,32,64,128]{3,2,1,0:T(8,128)(2,1)S(1)}, f16[2,32,64,128]{3,2,1,0:T(8,128)(2,1)S(1)}, u32[]{:S(2)}, u32[]{:S(2)}) %collective-permute-start.2) | collective-permute-done | bytes 1048608 | tf_op jit(solution)/shard_map/ppermute | solution.py:139
  69.1 0.3 convert_multiply_fusion.refs_1_
  69.3 17.2 %finish.2.refs_2_ = f32[2,2,2048,256]{3,2,1,0:T(8,128)} custom-call(f32[2,32,64,128]{3,2,1,0:T(8,128)S(1)} %get-tuple-element.11.refs_0_, f32[2,32,64,128]{3,2,1,0:T(8,128)S(1)} %convert_multiply_fusion.refs_1_), custom_call_target="tpu_custom_call" | custom-call | flops 100000000 | bytes 8388608 | tf_op jit(solution)/shard_map/finish/pallas_call | solution.py:207
  86.5 3.4 %collective-permute-done.1 = f16[2,32,64,128]{3,2,1,0:T(8,128)(2,1)S(1)} collective-permute-done((f16[2,32,64,128]{3,2,1,0:T(8,128)(2,1)S(1)}, f16[2,32,64,128]{3,2,1,0:T(8,128)(2,1)S(1)}, u32[]{:S(2)}, u32[]{:S(2)}) %collective-permute-start.1) | collective-permute-done | bytes 1048608 | tf_op jit(solution)/shard_map/ppermute | solution.py:139
  89.9 0.3 convert_multiply_fusion.1.refs_1_
  90.2 17.2 %finish.3 = f32[2,2,2048,256]{3,2,1,0:T(8,128)} custom-call(f32[2,32,64,128]{3,2,1,0:T(8,128)S(1)} %get-tuple-element.9.refs_0_, f32[2,32,64,128]{3,2,1,0:T(8,128)S(1)} %convert_multiply_fusion.1.refs_1_, f32[2,2,2048,256]{3,2,1,0:T(8,128)} %finish.2.refs_2_), custom_call_target="tpu_custom_call", output_to_operand_aliasing={{}: (2, {})} | custom-call | flops 100000000 | bytes 8388608 | tf_op jit(solution)/shard_map/finish/pallas_call | solution.py:207
  (4 shorter events, 0.0 us)
Async XLA Ops:
  0.0 12.2 %copy-start.4 = (bf16[512,768]{1,0:T(8,128)(2,1)S(1)}, bf16[512,768]{1,0:T(8,128)(2,1)}, u32[]{:S(2)}) copy-start(bf16[512,768]{1,0:T(8,128)(2,1)} %constant.27.clone) | copy-start | bytes 2359300
  0.0 12.2 %copy-start.3 = (f32[16,4096]{1,0:T(8,128)S(1)}, f32[16,4096]{1,0:T(8,128)}, u32[]{:S(2)}) copy-start(f32[16,4096]{1,0:T(8,128)} %param.7) | copy-start | bytes 786436
  6.1 17.2 %copy-start = (bf16[256,768]{1,0:T(8,128)(2,1)S(1)}, bf16[256,768]{1,0:T(8,128)(2,1)}, u32[]{:S(2)}) copy-start(bf16[256,768]{1,0:T(8,128)(2,1)} %constant.26.clone.first_ref) | copy-start | bytes 1179652
  6.1 17.2 %copy-start.1 = (f32[32,128]{1,0:T(8,128)S(1)}, f32[32,128]{1,0:T(8,128)}, u32[]{:S(2)}) copy-start(f32[32,128]{1,0:T(8,128)} %constant.25.clone.sin_ref) | copy-start | bytes 49156
  6.1 17.2 %copy-start.2 = (f32[32,128]{1,0:T(8,128)S(1)}, f32[32,128]{1,0:T(8,128)}, u32[]{:S(2)}) copy-start(f32[32,128]{1,0:T(8,128)} %constant.24.clone.cos_ref) | copy-start | bytes 49156
  7.3 16.0 %collective-permute-start = (bf16[2,2,16,32,128]{4,3,2,1,0:T(8,128)(2,1)S(1)}, bf16[2,2,16,32,128]{4,3,2,1,0:T(8,128)(2,1)S(1)}, u32[]{:S(2)}, u32[]{:S(2)}) collective-permute-start(bf16[2,2,16,32,128]{4,3,2,1,0:T(8,128)(2,1)S(1)} %slice.4), channel_id=1, source_target_pairs={{0,1},{2,3},{4,5},{6,7},{8,9},{10,11},{12,13},{14,15},{16,17},{18,... | collective-permute-start | bytes 1572872 | tf_op jit(solution)/shard_map/ppermute | solution.py:151
  42.6 26.5 %collective-permute-start.2 = (f16[2,32,64,128]{3,2,1,0:T(8,128)(2,1)S(1)}, f16[2,32,64,128]{3,2,1,0:T(8,128)(2,1)S(1)}, u32[]{:S(2)}, u32[]{:S(2)}) collective-permute-start(f16[2,32,64,128]{3,2,1,0:T(8,128)(2,1)S(1)} %fusion.1), channel_id=1, source_target_pairs={{0,1},{1,0},{2,3},{3,2},{4,5},{5,4},{6,7},{7,6},{8,9},{9,8},{10,11... | collective-permute-start | bytes 3145736 | tf_op jit(solution)/shard_map/ppermute | solution.py:139
  64.4 25.5 %collective-permute-start.1 = (f16[2,32,64,128]{3,2,1,0:T(8,128)(2,1)S(1)}, f16[2,32,64,128]{3,2,1,0:T(8,128)(2,1)S(1)}, u32[]{:S(2)}, u32[]{:S(2)}) collective-permute-start(f16[2,32,64,128]{3,2,1,0:T(8,128)(2,1)S(1)} %fusion), channel_id=1, source_target_pairs={{0,1},{1,0},{2,3},{3,2},{4,5},{5,4},{6,7},{7,6},{8,9},{9,8},{10,11... | collective-permute-start | bytes 3145736 | tf_op jit(solution)/shard_map/ppermute | solution.py:139
where the time goes:
time: 108 us; the launch traced here: 107 us
  Pallas kernels  72.4 us (67%)
  waiting for transfers between devices  18.9 us (17%)
  starting transfers between devices  7.56 us (7%)
  local copies, waits for them, and re-layouts  7.34 us (7%)
  other arithmetic  1.09 us (1%)
    pallas_call x2, Pallas kernels, shards(): pl.pallas_call(functools.partial(transform_kernel, parts, frames, rows, d...  38 us
    pallas_call x2, Pallas kernels, shards(): pl.pallas_call(functools.partial(finish_kernel, parts, frames, rows, step...  34.4 us
    ppermute x1, waiting for transfers between devices, shards(): halo = lax.ppermute(x[:, :, frames - depth:], 'tm', route)  11 us
    ppermute x2, waiting for transfers between devices, sent(): return lax.ppermute(narrow, 'tm', route).astype(jnp.float32) * 0.5  7.92 us
    reshape x1, local copies, waits for them, and re-layouts, shards(): x = signal.reshape(streams, 2, frames, rows, LANES)  6.11 us
    ppermute x1, starting transfers between devices, shards(): halo = lax.ppermute(x[:, :, frames - depth:], 'tm', route)  4.9 us
    ppermute x2, starting transfers between devices, sent(): return lax.ppermute(narrow, 'tm', route).astype(jnp.float32) * 0.5  2.65 us
  transfers between devices with their start and end apart: 3, of which 3 were waited for; matrix products, arithmetic and copies ran while one was open for 1% of the time, Pallas kernels for 34%

commit v1 on v0

--- a/solution.py
+++ b/solution.py
@@ -115,7 +115,7 @@
     own_ref, away_refs, out_ref, turned = refs[0], refs[1:parts], refs[-2], refs[-1]
     me = lax.axis_index("tm")
 
-    @pl.loop(0, rows)
+    @pl.loop(0, rows, unroll=8)
     def _(c):
         data = [[own_ref[p, c] for p in range(2)]]
         for ref in away_refs:
@@ -148,7 +148,7 @@
     me = lax.axis_index("tm")
     x = signal.reshape(streams, 2, frames, rows, LANES)
     route = [(i, i + 1) for i in range(parts - 1)]
-    halo = lax.ppermute(x[:, :, frames - depth :], "tm", route)
+    halos = [lax.ppermute(x[s : s + 1, :, frames - depth :], "tm", route) for s in range(streams)]
     taps = taps.reshape(depth, rows, LANES)
     twist = angles(rows, LANES, channels)
     cos, sin = jnp.asarray(np.cos(twist), jnp.float32), jnp.asarray(np.sin(twist), jnp.float32)
@@ -166,8 +166,7 @@
             grid=(1,),
             in_specs=[
                 pl.BlockSpec((1, 2, frames, rows, LANES), pick),
-                pl.BlockSpec((1, 2, depth, rows, LANES), pick),
-                whole(taps), whole(first), whole(cos), whole(sin), whole(second),
+                whole(halos[s]), whole(taps), whole(first), whole(cos), whole(sin), whole(second),
             ],
             out_specs=[
                 pl.BlockSpec((2, rows, each, frames), lambda i: (0, 0, 0, 0)),
@@ -186,7 +185,7 @@
             compiler_params=pltpu.CompilerParams(vmem_limit_bytes=48 << 20),
             cost_estimate=pl.CostEstimate(flops=8 * 10**9, bytes_accessed=8 << 20, transcendentals=0),
             name="transform",
-        )(x, halo, taps, first, cos, sin, second)
+        )(x, halos[s], taps, first, cos, sin, second)
         owns.append(own)
         aways.append([
             sent(away[k - 1], [(i, (i + k) % parts) for i in range(parts)])

time: 108 us -> 92 us (0.85)
  Pallas kernels: 72.4 us -> 52.4 us
  waiting for transfers between devices: 18.9 us -> 22 us
  starting transfers between devices: 7.56 us -> 8.81 us
    pallas_call x2, Pallas kernels: 34.4 us -> 14.4 us  [shards(): pl.pallas_call(functools.partial(finish_kernel, parts, frames, rows, step...]
    ppermute x2, waiting for transfers between devices: 7.92 us -> 16.8 us  [sent(): return lax.ppermute(narrow, 'tm', route).astype(jnp.float32) * 0.5]
    ppermute x1 -> x2, waiting for transfers between devices: 11 us -> 5.22 us  [shards(): lax.ppermute(x[s:s + 1, :, frames - depth:], 'tm', route)]
    ppermute x1 -> x2, starting transfers between devices: 4.9 us -> 6.19 us  [shards(): lax.ppermute(x[s:s + 1, :, frames - depth:], 'tm', route)]
  transfers between devices with their start and end apart: 3 -> 4, of which waited for: 3 -> 3; matrix products, arithmetic and copies ran while one was open for 1% -> 1% of each run, Pallas kernels for 34% -> 49%
where the time goes in v1:
time: 92 us; the launch traced here: 91.7 us
  Pallas kernels  52.4 us (57%)
  waiting for transfers between devices  22 us (24%)
  starting transfers between devices  8.81 us (10%)
  local copies, waits for them, and re-layouts  7.33 us (8%)
  other arithmetic  1.09 us (1%)
    pallas_call x2, Pallas kernels, shards(): pl.pallas_call(functools.partial(transform_kernel, parts, frames, rows, d...  38 us
    ppermute x2, waiting for transfers between devices, sent(): return lax.ppermute(narrow, 'tm', route).astype(jnp.float32) * 0.5  16.8 us
    pallas_call x2, Pallas kernels, shards(): pl.pallas_call(functools.partial(finish_kernel, parts, frames, rows, step...  14.4 us
    ppermute x2, starting transfers between devices, shards(): lax.ppermute(x[s:s + 1, :, frames - depth:], 'tm', route)  6.19 us
    reshape x1, local copies, waits for them, and re-layouts, shards(): x = signal.reshape(streams, 2, frames, rows, LANES)  6.11 us
    ppermute x2, waiting for transfers between devices, shards(): lax.ppermute(x[s:s + 1, :, frames - depth:], 'tm', route)  5.22 us
    ppermute x2, starting transfers between devices, sent(): return lax.ppermute(narrow, 'tm', route).astype(jnp.float32) * 0.5  2.62 us
  transfers between devices with their start and end apart: 4, of which 3 were waited for; matrix products, arithmetic and copies ran while one was open for 1% of the time, Pallas kernels for 49%

profile of v1, /device:TPU:0, one launch (start us, length us, event | category | flops | bytes accessed | tf_op | source)
XLA Modules:
  0.0 91.7 jit_solution(11891468349066390697)
XLA Ops:
  0.0 6.1 %reshape.12.x_ref = bf16[2,2,128,32,128]{4,3,2,1,0:T(8,128)(2,1)} reshape(bf16[2,2,524288]{2,1,0:T(2,128)(2,1)} %param.6) | data formatting | bytes 8388608 | tf_op jit(solution)/shard_map/reshape | solution.py:149
  6.1 1.1 %fusion.2 = (bf16[1,2,16,32,128]{4,3,2,1,0:T(8,128)(2,1)S(1)}, bf16[1,2,16,32,128]{4,3,2,1,0:T(8,128)(2,1)S(1)}) fusion(bf16[2,2,128,32,128]{4,3,2,1,0:T(8,128)(2,1)} %reshape.12.x_ref), kind=kLoop, calls=%fused_computation.7 | loop fusion | bytes 1048576 | tf_op jit(solution)/shard_map/slice | solution.py:151
  7.2 4.9 %collective-permute-start.2 = (bf16[1,2,16,32,128]{4,3,2,1,0:T(8,128)(2,1)S(1)}, bf16[1,2,16,32,128]{4,3,2,1,0:T(8,128)(2,1)S(1)}, u32[]{:S(2)}, u32[]{:S(2)}) collective-permute-start(bf16[1,2,16,32,128]{4,3,2,1,0:T(8,128)(2,1)S(1)} %get-tuple-element.13), channel_id=1, source_target_pairs={{0,1},{2,3},{4,5},{6,7},{8,9},{10,11},{12,13},{14,15},{16,17},{18,... | collective-permute-start | bytes 786440 | tf_op jit(solution)/shard_map/ppermute | solution.py:151
  12.1 1.3 %collective-permute-start = (bf16[1,2,16,32,128]{4,3,2,1,0:T(8,128)(2,1)S(1)}, bf16[1,2,16,32,128]{4,3,2,1,0:T(8,128)(2,1)S(1)}, u32[]{:S(2)}, u32[]{:S(2)}) collective-permute-start(bf16[1,2,16,32,128]{4,3,2,1,0:T(8,128)(2,1)S(1)} %get-tuple-element.14), channel_id=1, source_target_pairs={{0,1},{2,3},{4,5},{6,7},{8,9},{10,11},{12,13},{14,15},{16,17},{18,... | collective-permute-start | bytes 786440 | tf_op jit(solution)/shard_map/ppermute | solution.py:151
  13.5 0.0 copy-done.3
  13.5 0.1 copy.8
  13.5 0.0 copy-done.4
  13.6 5.2 %collective-permute-done.2.halo_ref = bf16[1,2,16,32,128]{4,3,2,1,0:T(8,128)(2,1)S(1)} collective-permute-done((bf16[1,2,16,32,128]{4,3,2,1,0:T(8,128)(2,1)S(1)}, bf16[1,2,16,32,128]{4,3,2,1,0:T(8,128)(2,1)S(1)}, u32[]{:S(2)}, u32[]{:S(2)}) %collective-permute-start.2) | collective-permute-done | bytes 262176 | tf_op jit(solution)/shard_map/ppermute | solution.py:151
  18.8 0.0 copy-done
  18.8 0.0 copy-done.1
  18.8 0.0 copy-done.2
  18.8 19.0 %transform.3 = (f32[2,32,64,128]{3,2,1,0:T(8,128)S(1)}, f32[1,2,32,64,128]{4,3,2,1,0:T(8,128)S(1)}) custom-call(bf16[2,2,128,32,128]{4,3,2,1,0:T(8,128)(2,1)} %reshape.12.x_ref, bf16[1,2,16,32,128]{4,3,2,1,0:T(8,128)(2,1)S(1)} %collective-permute-done.2.halo_ref, f32[16,32,128]{2,1,0:T(8,128)S(1)} %bitcast.6, bf16[256,768]{1,0:T(8,128)(2,1)S(1)} %copy-done, ...), custom_call_target="tpu_custom_call" | custom-call | flops 8000000000 | bytes 8388608 | tf_op jit(solution)/shard_map/transform/pallas_call | solution.py:164
  37.8 0.3 fusion.1
  38.1 2.5 %collective-permute-start.3 = (f16[2,32,64,128]{3,2,1,0:T(8,128)(2,1)S(1)}, f16[2,32,64,128]{3,2,1,0:T(8,128)(2,1)S(1)}, u32[]{:S(2)}, u32[]{:S(2)}) collective-permute-start(f16[2,32,64,128]{3,2,1,0:T(8,128)(2,1)S(1)} %fusion.1), channel_id=1, source_target_pairs={{0,1},{1,0},{2,3},{3,2},{4,5},{5,4},{6,7},{7,6},{8,9},{9,8},{10,11... | collective-permute-start | bytes 3145736 | tf_op jit(solution)/shard_map/ppermute | solution.py:139
  40.6 0.0 collective-permute-done.halo_ref
  40.6 19.0 %transform.2 = (f32[2,32,64,128]{3,2,1,0:T(8,128)S(1)}, f32[1,2,32,64,128]{4,3,2,1,0:T(8,128)S(1)}) custom-call(bf16[2,2,128,32,128]{4,3,2,1,0:T(8,128)(2,1)} %reshape.12.x_ref, bf16[1,2,16,32,128]{4,3,2,1,0:T(8,128)(2,1)S(1)} %collective-permute-done.halo_ref, f32[16,32,128]{2,1,0:T(8,128)S(1)} %bitcast.7, bf16[256,768]{1,0:T(8,128)(2,1)S(1)} %copy-done, ...), custom_call_target="tpu_custom_call" | custom-call | flops 8000000000 | bytes 8388608 | tf_op jit(solution)/shard_map/transform/pallas_call | solution.py:164
  59.7 0.3 fusion
  60.0 0.1 collective-permute-start.1
  60.0 4.1 %collective-permute-done.3 = f16[2,32,64,128]{3,2,1,0:T(8,128)(2,1)S(1)} collective-permute-done((f16[2,32,64,128]{3,2,1,0:T(8,128)(2,1)S(1)}, f16[2,32,64,128]{3,2,1,0:T(8,128)(2,1)S(1)}, u32[]{:S(2)}, u32[]{:S(2)}) %collective-permute-start.3) | collective-permute-done | bytes 1048608 | tf_op jit(solution)/shard_map/ppermute | solution.py:139
  64.1 0.3 convert_multiply_fusion.refs_1_
  64.4 7.2 %finish.2.refs_2_ = f32[2,2,2048,256]{3,2,1,0:T(8,128)} custom-call(f32[2,32,64,128]{3,2,1,0:T(8,128)S(1)} %get-tuple-element.11.refs_0_, f32[2,32,64,128]{3,2,1,0:T(8,128)S(1)} %convert_multiply_fusion.refs_1_), custom_call_target="tpu_custom_call" | custom-call | flops 100000000 | bytes 8388608 | tf_op jit(solution)/shard_map/finish/pallas_call | solution.py:206
  71.6 12.7 %collective-permute-done.1 = f16[2,32,64,128]{3,2,1,0:T(8,128)(2,1)S(1)} collective-permute-done((f16[2,32,64,128]{3,2,1,0:T(8,128)(2,1)S(1)}, f16[2,32,64,128]{3,2,1,0:T(8,128)(2,1)S(1)}, u32[]{:S(2)}, u32[]{:S(2)}) %collective-permute-start.1) | collective-permute-done | bytes 1048608 | tf_op jit(solution)/shard_map/ppermute | solution.py:139
  84.3 0.3 convert_multiply_fusion.1.refs_1_
  84.5 7.2 %finish.3 = f32[2,2,2048,256]{3,2,1,0:T(8,128)} custom-call(f32[2,32,64,128]{3,2,1,0:T(8,128)S(1)} %get-tuple-element.9.refs_0_, f32[2,32,64,128]{3,2,1,0:T(8,128)S(1)} %convert_multiply_fusion.1.refs_1_, f32[2,2,2048,256]{3,2,1,0:T(8,128)} %finish.2.refs_2_), custom_call_target="tpu_custom_call", output_to_operand_aliasing={{}: (2, {})} | custom-call | flops 100000000 | bytes 8388608 | tf_op jit(solution)/shard_map/finish/pallas_call | solution.py:206
  (6 shorter events, 0.0 us)
Async XLA Ops:
  0.0 13.5 %copy-start.4 = (bf16[512,768]{1,0:T(8,128)(2,1)S(1)}, bf16[512,768]{1,0:T(8,128)(2,1)}, u32[]{:S(2)}) copy-start(bf16[512,768]{1,0:T(8,128)(2,1)} %constant.27.clone) | copy-start | bytes 2359300
  0.0 13.5 %copy-start.3 = (f32[16,4096]{1,0:T(8,128)S(1)}, f32[16,4096]{1,0:T(8,128)}, u32[]{:S(2)}) copy-start(f32[16,4096]{1,0:T(8,128)} %param.7) | copy-start | bytes 786436
  6.1 12.7 %copy-start = (bf16[256,768]{1,0:T(8,128)(2,1)S(1)}, bf16[256,768]{1,0:T(8,128)(2,1)}, u32[]{:S(2)}) copy-start(bf16[256,768]{1,0:T(8,128)(2,1)} %constant.26.clone.first_ref) | copy-start | bytes 1179652
  6.1 12.7 %copy-start.1 = (f32[32,128]{1,0:T(8,128)S(1)}, f32[32,128]{1,0:T(8,128)}, u32[]{:S(2)}) copy-start(f32[32,128]{1,0:T(8,128)} %constant.25.clone.sin_ref) | copy-start | bytes 49156
  6.1 12.7 %copy-start.2 = (f32[32,128]{1,0:T(8,128)S(1)}, f32[32,128]{1,0:T(8,128)}, u32[]{:S(2)}) copy-start(f32[32,128]{1,0:T(8,128)} %constant.24.clone.cos_ref) | copy-start | bytes 49156
  7.2 11.6 %collective-permute-start.2 = (bf16[1,2,16,32,128]{4,3,2,1,0:T(8,128)(2,1)S(1)}, bf16[1,2,16,32,128]{4,3,2,1,0:T(8,128)(2,1)S(1)}, u32[]{:S(2)}, u32[]{:S(2)}) collective-permute-start(bf16[1,2,16,32,128]{4,3,2,1,0:T(8,128)(2,1)S(1)} %get-tuple-element.13), channel_id=1, source_target_pairs={{0,1},{2,3},{4,5},{6,7},{8,9},{10,11},{12,13},{14,15},{16,17},{18,... | collective-permute-start | bytes 786440 | tf_op jit(solution)/shard_map/ppermute | solution.py:151
  12.1 28.5 %collective-permute-start = (bf16[1,2,16,32,128]{4,3,2,1,0:T(8,128)(2,1)S(1)}, bf16[1,2,16,32,128]{4,3,2,1,0:T(8,128)(2,1)S(1)}, u32[]{:S(2)}, u32[]{:S(2)}) collective-permute-start(bf16[1,2,16,32,128]{4,3,2,1,0:T(8,128)(2,1)S(1)} %get-tuple-element.14), channel_id=1, source_target_pairs={{0,1},{2,3},{4,5},{6,7},{8,9},{10,11},{12,13},{14,15},{16,17},{18,... | collective-permute-start | bytes 786440 | tf_op jit(solution)/shard_map/ppermute | solution.py:151
  38.1 26.0 %collective-permute-start.3 = (f16[2,32,64,128]{3,2,1,0:T(8,128)(2,1)S(1)}, f16[2,32,64,128]{3,2,1,0:T(8,128)(2,1)S(1)}, u32[]{:S(2)}, u32[]{:S(2)}) collective-permute-start(f16[2,32,64,128]{3,2,1,0:T(8,128)(2,1)S(1)} %fusion.1), channel_id=1, source_target_pairs={{0,1},{1,0},{2,3},{3,2},{4,5},{5,4},{6,7},{7,6},{8,9},{9,8},{10,11... | collective-permute-start | bytes 3145736 | tf_op jit(solution)/shard_map/ppermute | solution.py:139
  60.0 24.3 %collective-permute-start.1 = (f16[2,32,64,128]{3,2,1,0:T(8,128)(2,1)S(1)}, f16[2,32,64,128]{3,2,1,0:T(8,128)(2,1)S(1)}, u32[]{:S(2)}, u32[]{:S(2)}) collective-permute-start(f16[2,32,64,128]{3,2,1,0:T(8,128)(2,1)S(1)} %fusion), channel_id=1, source_target_pairs={{0,1},{1,0},{2,3},{3,2},{4,5},{5,4},{6,7},{7,6},{8,9},{9,8},{10,11... | collective-permute-start | bytes 3145736 | tf_op jit(solution)/shard_map/ppermute | solution.py:139
